TPU v7x, 32 devices: a 4x2x2 block of a 4x4x8 slice. The times are simulated.
32 devices in a mesh: dp: 4 (over y, z), tp: 8 (over x, core).
Axes of the slice: x: 4, y: 2, z: 2, core: 2. Of those that a mesh axis runs over, the one named last changes fastest.
The devices are a block of a 4x4x8 slice.
Arguments:
- hidden: bfloat16 [32, 9, 4096], P('dp'), parts along dimension 0
- draft_ids: int32 [32, 8], P('dp'), parts along dimension 0
- norm_gain: bfloat16 [4096], replicated
- head_w: bfloat16 [4096, 128256], P(None, 'tp')
Outputs:
- output 1: float32 [32, 8], P('dp'), parts along dimension 0
- output 2: float32 [32, 9], P('dp'), parts along dimension 0
- output 3: float32 [32, 9], P('dp'), parts along dimension 0
There are 4 independent parts. A program takes and returns all parts, laid end to end along the dimension named above; an argument that names none is the same for every part.
All inputs are finite; a program needn't handle non-finite values.
Results may differ from a plain program's by a relative error of at most 0.001.
Values sent between devices are 32-bit elements.
A program may use at most 768 MiB of HBM per device.

v0:
```python
import jax
import jax.numpy as jnp
from jax import lax
from jax.sharding import PartitionSpec as P

NORM_EPS = 1e-5


def rms_norm(hidden, norm_gain):
    wide_x = hidden.astype(jnp.float32)
    inv_rms = lax.rsqrt(jnp.mean(wide_x * wide_x, axis=-1, keepdims=True) + NORM_EPS)
    return (wide_x * inv_rms * norm_gain.astype(jnp.float32)).astype(jnp.bfloat16)


def solution(mesh):
    def per_device(hidden, draft_ids, norm_gain, head_w):
        normed = rms_norm(hidden, norm_gain)
        logits = jnp.einsum('btd,dv->btv', normed, head_w, preferred_element_type=jnp.float32)
        gathered = lax.all_gather(logits, 'tp')
        shards = gathered.shape[0]
        shard_cols = gathered.shape[3]
        drafts = draft_ids.shape[1]
        row_max = jnp.max(gathered, axis=(0, 3))
        shifted = gathered - row_max[None, :, :, None]
        exp_vals = jnp.exp(shifted)
        exp_sum = jnp.sum(exp_vals, axis=(0, 3))
        weighted = jnp.sum(exp_vals * shifted, axis=(0, 3))
        log_sum = jnp.log(exp_sum)
        log_norm = row_max + log_sum
        entropy = log_sum - weighted / exp_sum
        col_ids = lax.broadcasted_iota(jnp.int32, (shards, 1, 1, shard_cols), 0) * shard_cols + lax.broadcasted_iota(jnp.int32, (shards, 1, 1, shard_cols), 3)
        picked = jnp.sum(jnp.where(col_ids == draft_ids[None, :, :, None], gathered[:, :, :drafts], 0.0), axis=(0, 3))
        return picked - log_norm[:, :drafts], log_norm, entropy

    specs_in = (P('dp', None, None), P('dp', None), P(None), P(None, 'tp'))
    specs_out = (P('dp', None), P('dp', None), P('dp', None))
    return jax.shard_map(per_device, mesh=mesh, in_specs=specs_in, out_specs=specs_out, check_vma=False)
```

profile of v0, /device:TPU:81, one launch (start us, length us, event | category | flops | bytes accessed | tf_op | source)
XLA Modules:
  0.0 291.1 jit_solution(1142084183960970291)
XLA Ops:
  7.2 0.1 all-gather.3.cloned.1.call-start
  7.2 1.3 fusion.4
  8.5 0.7 convert_element_type.10
  9.2 0.0 copy-start
  9.2 50.5 %fusion = f32[8,9,16032]{2,0,1:T(8,128)} fusion(bf16[4096,16032]{0,1:T(8,128)(2,1)} %param.7, bf16[8,9,4096]{2,0,1:T(8,128)(2,1)} %param.4, f32[4096]{0:T(1024)S(1)} %convert_element_type.10, f32[8,9]{0,1:T(8,128)S(1)} %add_rsqrt_fusion), kind=kOutput, calls=%fused_computation | convolution fusion | flops 9457238016 | bytes 136557856 | tf_op jit(solution)/shard_map/btd,dv->btv/dot_general | solution.py:18
  59.7 0.1 all-gather.3.cloned.1.call-update
  59.8 0.0 copy-done
  59.8 0.1 copy.18
  59.9 0.1 iota_add_fusion
  60.0 174.9 %all-gather.3.cloned.1.call-done = f32[64,9,16032]{2,0,1:T(8,128)} async-done(((f32[8,9,16032]{2,0,1:T(8,128)}), f32[64,9,16032]{2,0,1:T(8,128)}) %all-gather.3.cloned.1.call-update) | async-done | bytes 36937744 | tf_op jit(solution)/shard_map/all_gather | solution.py:19
  234.9 13.5 %reduce = f32[64,9]{0,1:T(8,128)S(1)} reduce(f32[64,9,16032]{2,0,1:T(8,128)} %all-gather.3.cloned.1.call-done, f32[]{:T(128)} %constant.10.clone.1), dimensions={2}, to_apply=%region_2.0 | reduce | flops 9233856 | bytes 36940036 | tf_op jit(solution)/shard_map/reduce_max | solution.py:23
  248.4 0.1 reshape.32
  248.5 20.5 %fusion.2 = (f32[8,9]{0,1:T(8,128)S(1)}, f32[8,9]{0,1:T(8,128)S(1)}) fusion(f32[8,9]{0,1:T(8,128)S(1)} %reduce_max.9, f32[64,9,16032]{2,0,1:T(8,128)} %all-gather.3.cloned.1.call-done), kind=kLoop, calls=%fused_computation.4 | loop fusion | flops 36937584 | bytes 36938592 | tf_op jit(solution)/shard_map/reduce_sum | solution.py:27
  269.1 0.7 copy.22
  269.8 13.1 %fusion.3 = f32[8,8]{0,1:T(8,128)S(1)} fusion(f32[8,8,9,16032]{3,1,0,2:T(8,128)} %bitcast.9, s32[8,8]{0,1:T(8,128)S(1)} %copy.18, s32[8,16032]{1,0:T(8,128)S(1)} %iota_add_fusion), kind=kLoop, calls=%fused_computation.6 | loop fusion | flops 24625088 | bytes 33347072 | tf_op jit(solution)/shard_map/reduce_sum | solution.py:32
  282.9 0.7 copy.21
  283.6 0.7 copy.23
  (5 shorter events, 0.0 us)
Async XLA Ops:
  7.2 227.7 %all-gather.3.cloned.1.call-start = ((), (), s32[]{:S(2)}) async-start(), calls=%async_computation | async-start | bytes 41803776 | tf_op jit(solution)/shard_map/all_gather | solution.py:19
  9.2 50.6 %copy-start = (s32[8,8]{1,0:T(8,128)S(1)}, s32[8,8]{1,0:T(8,128)}, u32[]{:S(2)}) copy-start(s32[8,8]{1,0:T(8,128)} %param.5) | copy-start | bytes 772
Sparse Core Ops, SparseCore 0:
  59.9 174.9 all-gather.2
where the time goes:
time: 292 us; the launch traced here: 291 us
  waiting for transfers between devices  175 us (60%)
  matrix products  50.5 us (17%)
  other arithmetic  49.3 us (17%)
  between operations  14.1 us (5%)
    all_gather x1, waiting for transfers between devices, per_device(): gathered = lax.all_gather(logits, 'tp')  175 us
    dot_general x1, matrix products, per_device(): jnp.einsum('btd,dv->btv', normed, head_w, preferred_element_type=jnp.floa...  50.5 us
    reduce_sum x1, other arithmetic, per_device(): weighted = jnp.sum(exp_vals * shifted, axis=(0, 3))  20.5 us
    reduce_max x2, other arithmetic, per_device(): row_max = jnp.max(gathered, axis=(0, 3))  13.5 us
    reduce_sum x1, other arithmetic, per_device(): jnp.sum(jnp.where(col_ids == draft_ids[None, :, :, None], gathered[:, :,...  13.1 us
  transfers between devices with their start and end apart: 1, of which 1 were waited for; matrix products, arithmetic and copies ran while one was open for 0% of the time, Pallas kernels for 0%

commit v1 on v0

v1 whole, which is shorter than its diff:
```python
import functools

import jax
import jax.numpy as jnp
from jax import lax
from jax.experimental import pallas as pl
from jax.experimental.pallas import tpu as pltpu
from jax.sharding import PartitionSpec as P

NORM_EPS = 1e-5
BLOCK = 512
SLOTS = 11
LANES = 128
NT = (((1,), (1,)), ((), ()))
F32 = jnp.float32


def kernel(tp, hid_hbm, ids_hbm, gain_hbm, wt_hbm, logp_ref, norm_ref, ent_ref,
           hid, ids, gain, nb, ring, logits, msgs, hid_sem, ids_sem, gain_sem, ring_sem, send_sem, recv_sem):
    steps, seqs, dim = hid_hbm.shape
    drafts = ids_hbm.shape[1]
    rows = steps * seqs
    cols = wt_hbm.shape[0]
    full = cols // BLOCK
    tail = cols - full * BLOCK
    me = lax.axis_index('tp')

    copies = (pltpu.make_async_copy(hid_hbm, hid, hid_sem), pltpu.make_async_copy(gain_hbm, gain, gain_sem),
              pltpu.make_async_copy(ids_hbm, ids, ids_sem))
    for copy in copies:
        copy.start()

    def load(block, slot):
        return pltpu.make_async_copy(wt_hbm.at[pl.ds(pl.multiple_of(block * BLOCK, BLOCK), BLOCK)], ring.at[slot], ring_sem.at[slot])

    def load_tail(slot):
        return pltpu.make_async_copy(wt_hbm.at[pl.ds(full * BLOCK, tail)], ring.at[slot, pl.ds(0, tail)], ring_sem.at[slot])

    for b in range(SLOTS):
        load(b, b).start()

    barrier = pltpu.get_barrier_semaphore()
    for step in range(1, tp):
        pl.semaphore_signal(barrier, inc=1, device_id={'tp': lax.rem(me + step, tp)}, device_id_type=pl.DeviceIdType.MESH)

    for copy in copies:
        copy.wait()

    nb[...] = jnp.zeros_like(nb)
    g = jnp.concatenate([gain[j:j + 1].astype(F32) for j in range(dim // LANES)], axis=1)

    def normed(t):
        x = hid[t].astype(F32)
        inv = lax.rsqrt(jnp.mean(x * x, axis=-1, keepdims=True) + NORM_EPS)
        return x * inv * g

    for t in range(0, steps - 1, 2):
        nb[pl.ds(t * seqs, 2 * seqs), :] = jnp.concatenate([normed(t), normed(t + 1)], axis=0).astype(jnp.bfloat16)
    if steps % 2:
        last = normed(steps - 1)
        nb[pl.ds((steps - 1) * seqs, 2 * seqs), :] = jnp.concatenate([last, jnp.zeros_like(last)], axis=0).astype(jnp.bfloat16)

    lane = lax.broadcasted_iota(jnp.int32, (seqs, LANES), 1)
    sub = lax.broadcasted_iota(jnp.int32, (seqs, LANES), 0)
    spread = jnp.full((seqs, LANES), -1, jnp.int32)
    for t in range(drafts):
        spread = jnp.where(lane // seqs == t, ids[:, t:t + 1] - me * cols, spread)
    spread = jnp.sum(jnp.where(lane % seqs == sub, spread, 0), axis=0, keepdims=True)
    id_row = jnp.where(lane[:1] < drafts * seqs, spread, -1)
    id_rel = jnp.broadcast_to(id_row, (seqs, LANES)) - sub

    def stats(carry, first, count):
        m, s, w, p = carry
        z = [logits[pl.ds(8 * j, 8), :] for j in range(count // 8)]
        tree = list(z)
        while len(tree) > 1:
            tree = [jnp.maximum(tree[i], tree[i + 1]) if i + 1 < len(tree) else tree[i] for i in range(0, len(tree), 2)]
        top = jnp.maximum(m, tree[0])
        drop = m - top
        keep = jnp.exp(drop)
        w = keep * (w + s * drop)
        s = s * keep
        off = id_rel - first
        for j in range(count // 8):
            d = z[j] - top
            e = jnp.exp(d)
            s = s + e
            w = w + e * d
            p = p + jnp.where(off == 8 * j, z[j], 0.0)
        return top, s, w, p

    low = jnp.full((8, LANES), -1e30, F32)
    zero = jnp.zeros((8, LANES), F32)

    def block_step(i, carry):
        slot = lax.rem(i, SLOTS)
        load(i, slot).wait()
        logits[...] = lax.dot_general(ring[slot], nb[...], NT, preferred_element_type=F32)
        ahead = i + SLOTS

        @pl.when(ahead < full)
        def _():
            load(ahead, slot).start()

        @pl.when(ahead == full)
        def _():
            load_tail(slot).start()

        return stats(carry, i * BLOCK, BLOCK)

    m, s, w, p = lax.fori_loop(0, full, block_step, (low, zero, zero, zero))
    slot = full % SLOTS
    load_tail(slot).wait()
    logits[pl.ds(0, tail), :] = lax.dot_general(ring[slot, 0:tail], nb[...], NT, preferred_element_type=F32)
    m, s, w, p = stats((m, s, w, p), full * BLOCK, tail)

    top = jnp.max(m, axis=0, keepdims=True)
    drop = m - top
    keep = jnp.exp(drop)
    w = jnp.sum(keep * (w + s * drop), axis=0, keepdims=True)
    s = jnp.sum(keep * s, axis=0, keepdims=True)
    p = jnp.sum(p, axis=0, keepdims=True)
    own = jnp.where(sub == 0, top, jnp.where(sub == 1, s, jnp.where(sub == 2, w, jnp.where(sub == 3, p, 0.0))))
    msgs[me] = own

    pl.semaphore_wait(barrier, tp - 1)

    def send(step):
        return pltpu.make_async_remote_copy(
            src_ref=msgs.at[me], dst_ref=msgs.at[me], send_sem=send_sem.at[step], recv_sem=recv_sem.at[step],
            device_id={'tp': lax.rem(me + step, tp)}, device_id_type=pl.DeviceIdType.MESH)

    def arrival(step):
        return pltpu.make_async_remote_copy(
            src_ref=msgs.at[me], dst_ref=msgs.at[lax.rem(me + tp - step, tp)], send_sem=send_sem.at[step], recv_sem=recv_sem.at[step],
            device_id={'tp': lax.rem(me + step, tp)}, device_id_type=pl.DeviceIdType.MESH)

    for step in range(1, tp):
        send(step).start()
    for step in range(1, tp):
        arrival(step).wait_recv()
    for step in range(1, tp):
        send(step).wait_send()

    parts = [msgs[k] for k in range(tp)]
    top = parts[0][0:1]
    for part in parts[1:]:
        top = jnp.maximum(top, part[0:1])
    s = jnp.zeros((1, LANES), F32)
    w = jnp.zeros((1, LANES), F32)
    p = jnp.zeros((1, LANES), F32)
    for part in parts:
        drop = part[0:1] - top
        keep = jnp.exp(drop)
        s = s + keep * part[1:2]
        w = w + keep * (part[2:3] + part[1:2] * drop)
        p = p + part[3:4]
    log_sum = jnp.log(s)
    log_norm = top + log_sum
    entropy = log_sum - w / s
    logp = p - log_norm

    def place(row, count):
        grid = jnp.where(lane % seqs == sub, jnp.broadcast_to(row, (seqs, LANES)), 0.0)
        out = jnp.zeros((seqs, LANES), F32)
        for t in range(count):
            col = jnp.sum(jnp.where(lane // seqs == t, grid, 0.0), axis=1, keepdims=True)
            out = jnp.where(lane == t, col, out)
        return out[:, 0:count]

    logp_ref[...] = place(logp, drafts)
    norm_ref[...] = place(log_norm, steps)
    ent_ref[...] = place(entropy, steps)


def solution(mesh):
    tp = mesh.shape['tp']

    def per_device(hidden, draft_ids, norm_gain, head_w):
        seqs, steps, dim = hidden.shape
        cols = head_w.shape[1]
        drafts = draft_ids.shape[1]
        anywhere = pl.BlockSpec(memory_space=pl.ANY)
        vmem = pl.BlockSpec(memory_space=pltpu.VMEM)
        return pl.pallas_call(
            functools.partial(kernel, tp),
            in_specs=[anywhere] * 4,
            out_specs=[vmem] * 3,
            out_shape=[jax.ShapeDtypeStruct((seqs, drafts), F32), jax.ShapeDtypeStruct((seqs, steps), F32),
                       jax.ShapeDtypeStruct((seqs, steps), F32)],
            scratch_shapes=[
                pltpu.VMEM((steps, seqs, dim), jnp.bfloat16),
                pltpu.VMEM((seqs, drafts), jnp.int32),
                pltpu.VMEM((dim // LANES, LANES), jnp.bfloat16),
                pltpu.VMEM((LANES, dim), jnp.bfloat16),
                pltpu.VMEM((SLOTS, BLOCK, dim), jnp.bfloat16),
                pltpu.VMEM((BLOCK, LANES), F32),
                pltpu.VMEM((tp, 8, LANES), F32),
                pltpu.SemaphoreType.DMA, pltpu.SemaphoreType.DMA, pltpu.SemaphoreType.DMA,
                pltpu.SemaphoreType.DMA((SLOTS,)),
                pltpu.SemaphoreType.DMA((tp,)),
                pltpu.SemaphoreType.DMA((tp,)),
            ],
            compiler_params=pltpu.CompilerParams(collective_id=0, has_side_effects=True, vmem_limit_bytes=60 * 2**20),
        )(hidden.transpose(1, 0, 2), draft_ids, norm_gain.reshape(dim // LANES, LANES), head_w.T)

    specs_in = (P('dp', None, None), P('dp', None), P(None), P(None, 'tp'))
    specs_out = (P('dp', None), P('dp', None), P('dp', None))
    return jax.shard_map(per_device, mesh=mesh, in_specs=specs_in, out_specs=specs_out, check_vma=False)
```

time: 292 us -> 67.3 us (0.23)
  waiting for transfers between devices: 175 us -> 0 us
  Pallas kernels: 0 us -> 62.7 us
  matrix products: 50.5 us -> 0 us
  other arithmetic: 49.3 us -> 0 us
  between operations: 14.1 us -> 0.64 us
    all_gather x1 -> x0, waiting for transfers between devices: 175 us -> none  [per_device(): gathered = lax.all_gather(logits, 'tp')]
    pallas_call x0 -> x1, Pallas kernels: none -> 62.7 us  [per_device(): pl.pallas_call(functools.partial(kernel, tp), in_specs=[anywhere] * 4, ou...]
    dot_general x1 -> x0, matrix products: 50.5 us -> none  [per_device(): jnp.einsum('btd,dv->btv', normed, head_w, preferred_element_type=jnp.floa...]
    reduce_sum x3 -> x0, other arithmetic: 34.9 us -> none  [the longest x1 20.5 us: per_device(): weighted = jnp.sum(exp_vals * shifted, axis=(0, 3))]
    reduce_max x2 -> x0, other arithmetic: 13.5 us -> none  [per_device(): row_max = jnp.max(gathered, axis=(0, 3))]
  transfers between devices with their start and end apart: 1 -> 0, of which waited for: 1 -> 0; matrix products, arithmetic and copies ran while one was open for 0% -> 0% of each run, Pallas kernels for 0% -> 0%
where the time goes in v1:
time: 67.3 us; the launch traced here: 67.1 us
  Pallas kernels  62.7 us (93%)
  local copies, waits for them, and re-layouts  3.8 us (6%)
    pallas_call x1, Pallas kernels, per_device(): pl.pallas_call(functools.partial(kernel, tp), in_specs=[anywhere] * 4, ou...  62.7 us
    unnamed x3, local copies, waits for them, and re-layouts  3.8 us

profile of v1, /device:TPU:81, one launch (start us, length us, event | category | flops | bytes accessed | tf_op | source)
XLA Modules:
  0.0 67.1 jit_solution(6722937905301122351)
XLA Ops:
  0.6 62.7 %shard_map.67 = (f32[8,8]{1,0:T(8,128)}, f32[8,9]{1,0:T(8,128)}, f32[8,9]{1,0:T(8,128)}) custom-call(bf16[9,8,4096]{2,1,0:T(8,128)(2,1)} %bitcast.3, s32[8,8]{1,0:T(8,128)} %ids_hbm.1, bf16[32,128]{1,0:T(8,128)(2,1)} %bitcast.4, bf16[16032,4096]{1,0:T(8,128)(2,1)} %bitcast.2.wt_hbm), custom_call_target="tpu_custom_call" | custom-call | tf_op jit(solution)/shard_map/pallas_call | solution.py:185
  63.3 1.3 %copy.10 = f32[8,8]{1,0:T(8,128)} copy(f32[8,8]{1,0:T(8,128)} %get-tuple-element.6) | data formatting | bytes 512
  64.6 1.3 %copy.11 = f32[8,9]{1,0:T(8,128)} copy(f32[8,9]{1,0:T(8,128)} %get-tuple-element.7) | data formatting | bytes 576
  65.8 1.3 %copy.12 = f32[8,9]{1,0:T(8,128)} copy(f32[8,9]{1,0:T(8,128)} %get-tuple-element.8) | data formatting | bytes 576

commit v2 on v1

v2 whole, which is shorter than its diff:
```python
import functools

import jax
import jax.numpy as jnp
from jax import lax
from jax.experimental import pallas as pl
from jax.experimental.pallas import tpu as pltpu
from jax.sharding import PartitionSpec as P

NORM_EPS = 1e-5
BLOCK = 512
SLOTS = 4
ALONE = 12
PIECES = 4
LANES = 128
NT = (((1,), (1,)), ((), ()))
F32 = jnp.float32
MESH = pl.DeviceIdType.MESH


def kernel(tp, hid_hbm, ids_hbm, gain_hbm, wt_hbm, out_ref,
           hid, ids, far_ids, gain, near_f32, far_f32, nb, ring, logits, msgs,
           hid_sem, ids_sem, gain_sem, ring_sem, z_send, z_recv, d_send, d_recv, i_send, i_recv, send_sem, recv_sem):
    steps, seqs, dim = hid_hbm.shape
    drafts = ids_hbm.shape[1]
    rows = steps * seqs
    cols = wt_hbm.shape[0]
    alone = ALONE * BLOCK
    share = (cols - alone) // 2
    blocks = ALONE + share // BLOCK
    tail = share % BLOCK
    group, me = lax.axis_index('dp'), lax.axis_index('tp')
    side = lax.rem(group, 2)
    mate = group + 1 - 2 * side
    core = lax.rem(me, 2)
    twin = me + 1 - 2 * core

    copies = (pltpu.make_async_copy(hid_hbm, hid, hid_sem), pltpu.make_async_copy(gain_hbm, gain, gain_sem),
              pltpu.make_async_copy(ids_hbm, ids, ids_sem))
    for copy in copies:
        copy.start()

    def first_col(block):
        return pl.multiple_of(block * BLOCK + jnp.where(block >= ALONE, side * share, 0), 16)

    def load(block, slot):
        return pltpu.make_async_copy(wt_hbm.at[pl.ds(first_col(block), BLOCK)], ring.at[slot], ring_sem.at[slot])

    def load_tail(slot):
        return pltpu.make_async_copy(wt_hbm.at[pl.ds(first_col(jnp.int32(blocks)), tail)], ring.at[slot, pl.ds(0, tail)], ring_sem.at[slot])

    for b in range(SLOTS):
        load(b, b).start()

    def peers():
        for k in range(1, tp):
            yield group, lax.rem(me + k, tp)
        for k in range(tp):
            yield mate, lax.rem(me + k, tp)

    barrier = pltpu.get_barrier_semaphore()
    for g, t in peers():
        pl.semaphore_signal(barrier, inc=1, device_id={'dp': g, 'tp': t}, device_id_type=MESH)

    for copy in copies:
        copy.wait()

    scale = jnp.concatenate([gain[j:j + 1].astype(F32) for j in range(dim // LANES)], axis=1)
    for t in range(steps):
        x = hid[t].astype(F32)
        inv = lax.rsqrt(jnp.mean(x * x, axis=-1, keepdims=True) + NORM_EPS)
        near_f32[pl.ds(t * seqs, seqs), :] = (x * inv * scale).astype(jnp.bfloat16).astype(F32)

    pl.semaphore_wait(barrier, 2 * tp - 1)

    half = dim // 2
    width = half // PIECES

    def columns(c, k):
        return pl.ds(pl.multiple_of(c * half + k * width, LANES), width)

    def across(k):
        return pltpu.make_async_remote_copy(
            src_ref=near_f32.at[:, columns(core, k)], dst_ref=far_f32.at[:, columns(core, k)],
            send_sem=z_send.at[k], recv_sem=z_recv.at[k], device_id={'dp': mate, 'tp': me}, device_id_type=MESH)

    def onward(k):
        return pltpu.make_async_remote_copy(
            src_ref=far_f32.at[:, columns(core, k)], dst_ref=far_f32.at[:, columns(core, k)],
            send_sem=d_send.at[k], recv_sem=d_recv.at[k], device_id={'dp': group, 'tp': twin}, device_id_type=MESH)

    def landing(k):
        return pltpu.make_async_remote_copy(
            src_ref=far_f32.at[:, columns(core, k)], dst_ref=far_f32.at[:, columns(1 - core, k)],
            send_sem=d_send.at[k], recv_sem=d_recv.at[k], device_id={'dp': group, 'tp': twin}, device_id_type=MESH)

    ids_copy = pltpu.make_async_remote_copy(src_ref=ids, dst_ref=far_ids, send_sem=i_send, recv_sem=i_recv,
                                            device_id={'dp': mate, 'tp': me}, device_id_type=MESH)
    ids_copy.start()
    for k in range(PIECES):
        across(k).start()

    nb[...] = jnp.zeros_like(nb)
    whole = rows // 16 * 16

    def pack(base, src):
        nb[pl.ds(base, whole), :] = src[0:whole, :].astype(jnp.bfloat16)
        rest = src[whole:rows, :]
        nb[pl.ds(base + whole, 16), :] = jnp.concatenate([rest, jnp.zeros_like(rest)], axis=0).astype(jnp.bfloat16)

    pack(0, near_f32)

    lane = lax.broadcasted_iota(jnp.int32, (seqs, LANES), 1)
    sub = lax.broadcasted_iota(jnp.int32, (seqs, LANES), 0)

    def id_grid(src):
        spread = jnp.full((seqs, LANES), -1, jnp.int32)
        for t in range(drafts):
            spread = jnp.where(lane // seqs == t, src[:, t:t + 1] - me * cols, spread)
        row = jnp.sum(jnp.where(lane % seqs == sub, spread, 0), axis=0, keepdims=True)
        return jnp.broadcast_to(jnp.where(lane[:1] < drafts * seqs, row, -1), (seqs, LANES)) - sub

    def stats(carry, id_rel, buf, base, first, count):
        m, s, w, p = carry
        z = [logits[buf, pl.ds(8 * j, 8), base:base + LANES] for j in range(count // 8)]
        tree = list(z)
        while len(tree) > 1:
            tree = [jnp.maximum(tree[i], tree[i + 1]) if i + 1 < len(tree) else tree[i] for i in range(0, len(tree), 2)]
        top = jnp.maximum(m, tree[0])
        drop = m - top
        keep = jnp.exp(drop)
        w = keep * (w + s * drop)
        s = s * keep
        off = id_rel - first
        for j in range(count // 8):
            d = z[j] - top
            e = jnp.exp(d)
            s = s + e
            w = w + e * d
            p = p + jnp.where(off == 8 * j, z[j], 0.0)
        return top, s, w, p

    low = jnp.full((8, LANES), -1e30, F32)
    zero = jnp.zeros((8, LANES), F32)
    fresh = (low, zero, zero, zero)
    near_id = id_grid(ids)

    def refill(block, slot):
        @pl.when(block < blocks)
        def _():
            load(block, slot).start()

        @pl.when(block == blocks)
        def _():
            load_tail(slot).start()

    def pair(block, near, far=None, second=BLOCK):
        wide = LANES if far is None else 2 * LANES
        counts = (BLOCK, second)
        slots = [lax.rem(block + u, SLOTS) for u in range(2)]
        load(block, slots[0]).wait()
        if second == BLOCK:
            load(block + 1, slots[1]).wait()
        else:
            load_tail(slots[1]).wait()
        for u in range(2):
            logits[u, 0:counts[u], 0:wide] = lax.dot_general(ring[slots[u], 0:counts[u]], nb[0:wide], NT, preferred_element_type=F32)
        for u in range(2):
            refill(block + u + SLOTS, slots[u])
        for u in range(2):
            first = first_col(block + u)
            near = stats(near, near_id, u, 0, first, counts[u])
            if far is not None:
                far = stats(far, far_id, u, LANES, first, counts[u])
        return near, far

    near = lax.fori_loop(0, ALONE // 2, lambda i, c: pair(2 * i, c)[0], fresh)
    for k in range(PIECES):
        across(k).wait_recv()
        onward(k).start()
    ids_copy.wait_recv()
    far_id = id_grid(far_ids)
    for k in range(PIECES):
        landing(k).wait_recv()
    pack(LANES, far_f32)

    together = blocks - ALONE
    near, far = lax.fori_loop(0, together // 2, lambda i, c: pair(ALONE + 2 * i, *c), (near, fresh))
    near, far = pair(jnp.int32(blocks - 1), near, far, tail)

    def fold(carry):
        m, s, w, p = carry
        top = jnp.max(m, axis=0, keepdims=True)
        drop = m - top
        keep = jnp.exp(drop)
        w = jnp.sum(keep * (w + s * drop), axis=0, keepdims=True)
        s = jnp.sum(keep * s, axis=0, keepdims=True)
        p = jnp.sum(p, axis=0, keepdims=True)
        return jnp.where(sub == 0, top, jnp.where(sub == 1, s, jnp.where(sub == 2, w, jnp.where(sub == 3, p, 0.0))))

    own = side * tp + me
    msgs[2 * tp] = fold(far)
    msgs[own] = fold(near)

    def send(k, g, t):
        here = k < tp
        return pltpu.make_async_remote_copy(
            src_ref=msgs.at[own if here else 2 * tp], dst_ref=msgs.at[own], send_sem=send_sem.at[k], recv_sem=recv_sem.at[k],
            device_id={'dp': g, 'tp': t}, device_id_type=MESH)

    sends = []
    for k in range(1, tp):
        sends.append(send(k, group, lax.rem(me + k, tp)))
    for k in range(tp):
        sends.append(send(tp + k, mate, lax.rem(me + k, tp)))
    for copy in reversed(sends):
        copy.start()

    def arrival(k):
        source = (side if k < tp else 1 - side) * tp + lax.rem(me + 2 * tp - k, tp)
        return pltpu.make_async_remote_copy(
            src_ref=msgs.at[own], dst_ref=msgs.at[source], send_sem=send_sem.at[k], recv_sem=recv_sem.at[k],
            device_id={'dp': group, 'tp': twin}, device_id_type=MESH)

    for k in range(1, 2 * tp):
        arrival(k).wait_recv()
    out_ref[...] = msgs[0:2 * tp]
    for copy in sends:
        copy.wait_send()
    for k in range(PIECES):
        across(k).wait_send()
        onward(k).wait_send()
    ids_copy.wait_send()


def finish(parts_ref, logp_ref, norm_ref, ent_ref):
    seqs, drafts = logp_ref.shape
    steps = norm_ref.shape[1]
    lane = lax.broadcasted_iota(jnp.int32, (seqs, LANES), 1)
    sub = lax.broadcasted_iota(jnp.int32, (seqs, LANES), 0)
    parts = [parts_ref[k] for k in range(parts_ref.shape[0])]
    top = parts[0][0:1]
    for part in parts[1:]:
        top = jnp.maximum(top, part[0:1])
    s = jnp.zeros((1, LANES), F32)
    w = jnp.zeros((1, LANES), F32)
    p = jnp.zeros((1, LANES), F32)
    for part in parts:
        drop = part[0:1] - top
        keep = jnp.exp(drop)
        s = s + keep * part[1:2]
        w = w + keep * (part[2:3] + part[1:2] * drop)
        p = p + part[3:4]
    log_sum = jnp.log(s)
    log_norm = top + log_sum
    entropy = log_sum - w / s
    logp = p - log_norm

    def place(row, count):
        grid = jnp.where(lane % seqs == sub, jnp.broadcast_to(row, (seqs, LANES)), 0.0)
        out = jnp.zeros((seqs, LANES), F32)
        for t in range(count):
            col = jnp.sum(jnp.where(lane // seqs == t, grid, 0.0), axis=1, keepdims=True)
            out = jnp.where(lane == t, col, out)
        return out[:, 0:count]

    logp_ref[...] = place(logp, drafts)
    norm_ref[...] = place(log_norm, steps)
    ent_ref[...] = place(entropy, steps)


def solution(mesh):
    tp = mesh.shape['tp']

    def per_device(hidden, draft_ids, norm_gain, head_w):
        seqs, steps, dim = hidden.shape
        rows = steps * seqs
        drafts = draft_ids.shape[1]
        anywhere = pl.BlockSpec(memory_space=pl.ANY)
        vmem = pl.BlockSpec(memory_space=pltpu.VMEM)
        dma = pltpu.SemaphoreType.DMA
        parts = pl.pallas_call(
            functools.partial(kernel, tp),
            in_specs=[anywhere] * 4,
            out_specs=vmem,
            out_shape=jax.ShapeDtypeStruct((2 * tp, 8, LANES), F32),
            scratch_shapes=[
                pltpu.VMEM((steps, seqs, dim), jnp.bfloat16),
                pltpu.VMEM((seqs, drafts), jnp.int32),
                pltpu.VMEM((seqs, drafts), jnp.int32),
                pltpu.VMEM((dim // LANES, LANES), jnp.bfloat16),
                pltpu.VMEM((rows, dim), F32),
                pltpu.VMEM((rows, dim), F32),
                pltpu.VMEM((2 * LANES, dim), jnp.bfloat16),
                pltpu.VMEM((SLOTS, BLOCK, dim), jnp.bfloat16),
                pltpu.VMEM((2, BLOCK, 2 * LANES), F32),
                pltpu.VMEM((2 * tp + 1, 8, LANES), F32),
                dma, dma, dma,
                dma((SLOTS,)),
                dma((PIECES,)), dma((PIECES,)), dma((PIECES,)), dma((PIECES,)),
                dma, dma,
                dma((2 * tp,)), dma((2 * tp,)),
            ],
            compiler_params=pltpu.CompilerParams(collective_id=0, has_side_effects=True, vmem_limit_bytes=60 * 2**20),
        )(hidden.transpose(1, 0, 2), draft_ids, norm_gain.reshape(dim // LANES, LANES), head_w.T)
        return pl.pallas_call(
            finish,
            in_specs=[vmem],
            out_specs=[vmem] * 3,
            out_shape=[jax.ShapeDtypeStruct((seqs, drafts), F32), jax.ShapeDtypeStruct((seqs, steps), F32),
                       jax.ShapeDtypeStruct((seqs, steps), F32)],
        )(parts)

    specs_in = (P('dp', None, None), P('dp', None), P(None), P(None, 'tp'))
    specs_out = (P('dp', None), P('dp', None), P('dp', None))
    return jax.shard_map(per_device, mesh=mesh, in_specs=specs_in, out_specs=specs_out, check_vma=False)
```

time: 67.3 us -> 48.9 us (0.73)
  Pallas kernels: 62.7 us -> 48.1 us
  local copies, waits for them, and re-layouts: 3.8 us -> 0 us
    pallas_call x1, Pallas kernels: 62.7 us -> 46.5 us  [per_device(): pl.pallas_call(functools.partial(kernel, tp), in_specs=[anywhere] * 4, ou...]
    unnamed x3 -> x0, local copies, waits for them, and re-layouts: 3.8 us -> none
    pallas_call x0 -> x1, Pallas kernels: none -> 1.59 us  [per_device(): pl.pallas_call(finish, in_specs=[vmem], out_specs=[vmem] * 3, out_shape=[...]
where the time goes in v2:
time: 48.9 us; the launch traced here: 48.8 us
  Pallas kernels  48.1 us (98%)
  between operations  0.64 us (1%)
    pallas_call x1, Pallas kernels, per_device(): pl.pallas_call(functools.partial(kernel, tp), in_specs=[anywhere] * 4, ou...  46.5 us
    pallas_call x1, Pallas kernels, per_device(): pl.pallas_call(finish, in_specs=[vmem], out_specs=[vmem] * 3, out_shape=[...  1.59 us

profile of v2, /device:TPU:81, one launch (start us, length us, event | category | flops | bytes accessed | tf_op | source)
XLA Modules:
  0.0 48.8 jit_solution(11669357997225624858)
XLA Ops:
  0.6 46.5 %shard_map.67.parts_ref = f32[16,8,128]{2,1,0:T(8,128)} custom-call(bf16[9,8,4096]{2,1,0:T(8,128)(2,1)} %bitcast.3, s32[8,8]{1,0:T(8,128)} %ids_hbm.1, bf16[32,128]{1,0:T(8,128)(2,1)} %bitcast.4, bf16[16032,4096]{1,0:T(8,128)(2,1)} %bitcast.2.wt_hbm), custom_call_target="tpu_custom_call" | custom-call | tf_op jit(solution)/shard_map/pallas_call | solution.py:282
  47.2 1.6 %shard_map.68 = (f32[8,8]{1,0:T(8,128)}, f32[8,9]{1,0:T(8,128)}, f32[8,9]{1,0:T(8,128)}) custom-call(f32[16,8,128]{2,1,0:T(8,128)} %shard_map.67.parts_ref), custom_call_target="tpu_custom_call" | custom-call | tf_op jit(solution)/shard_map/pallas_call | solution.py:306

commit v3 on v2

--- a/solution.py
+++ b/solution.py
@@ -9,9 +9,10 @@
 
 NORM_EPS = 1e-5
 BLOCK = 512
-SLOTS = 4
-ALONE = 12
-PIECES = 4
+SLOTS = 12
+ALONE = 8
+HALVES = 2
+TRIP = 4
 LANES = 128
 NT = (((1,), (1,)), ((), ()))
 F32 = jnp.float32
@@ -19,7 +20,7 @@
 
 
 def kernel(tp, hid_hbm, ids_hbm, gain_hbm, wt_hbm, out_ref,
-           hid, ids, far_ids, gain, near_f32, far_f32, nb, ring, logits, msgs,
+           hid, ids, far_ids, gain, near_f32, far_f32, nb, ring, logits, part, msgs,
            hid_sem, ids_sem, gain_sem, ring_sem, z_send, z_recv, d_send, d_recv, i_send, i_recv, send_sem, recv_sem):
     steps, seqs, dim = hid_hbm.shape
     drafts = ids_hbm.shape[1]
@@ -27,8 +28,12 @@
     cols = wt_hbm.shape[0]
     alone = ALONE * BLOCK
     share = (cols - alone) // 2
-    blocks = ALONE + share // BLOCK
     tail = share % BLOCK
+    sharing = share // BLOCK + (tail > 0)
+    last = tail or BLOCK
+    depth = dim // HALVES
+    lone = ALONE * HALVES
+    units = lone + sharing * HALVES
     group, me = lax.axis_index('dp'), lax.axis_index('tp')
     side = lax.rem(group, 2)
     mate = group + 1 - 2 * side
@@ -40,17 +45,31 @@
     for copy in copies:
         copy.start()
 
-    def first_col(block):
-        return pl.multiple_of(block * BLOCK + jnp.where(block >= ALONE, side * share, 0), 16)
-
-    def load(block, slot):
-        return pltpu.make_async_copy(wt_hbm.at[pl.ds(first_col(block), BLOCK)], ring.at[slot], ring_sem.at[slot])
-
-    def load_tail(slot):
-        return pltpu.make_async_copy(wt_hbm.at[pl.ds(first_col(jnp.int32(blocks)), tail)], ring.at[slot, pl.ds(0, tail)], ring_sem.at[slot])
-
-    for b in range(SLOTS):
-        load(b, b).start()
+    def place(unit):
+        own, far = unit < lone, unit - lone
+        half = jnp.where(own, lax.rem(unit, HALVES), far // sharing)
+        block = jnp.where(own, unit // HALVES, lax.rem(far, sharing))
+        col = block * BLOCK + jnp.where(own, 0, alone + side * share)
+        return pl.multiple_of(col, 16), pl.multiple_of(half * depth, LANES)
+
+    def load(unit, slot, count=BLOCK):
+        col, start = place(unit)
+        return pltpu.make_async_copy(wt_hbm.at[pl.ds(col, count), pl.ds(start, depth)], ring.at[slot, pl.ds(0, count)], ring_sem.at[slot])
+
+    def begin(unit, slot):
+        far = unit - lone
+        short = (far >= 0) & (lax.rem(far, sharing) == sharing - 1)
+
+        @pl.when((unit < units) & jnp.logical_not(short))
+        def _():
+            load(unit, slot).start()
+
+        @pl.when((unit < units) & short)
+        def _():
+            load(unit, slot, last).start()
+
+    for u in range(TRIP):
+        load(jnp.int32(u), u).start()
 
     def peers():
         for k in range(1, tp):
@@ -71,13 +90,14 @@
         inv = lax.rsqrt(jnp.mean(x * x, axis=-1, keepdims=True) + NORM_EPS)
         near_f32[pl.ds(t * seqs, seqs), :] = (x * inv * scale).astype(jnp.bfloat16).astype(F32)
 
+    for u in range(TRIP, SLOTS - TRIP):
+        load(jnp.int32(u), u).start()
     pl.semaphore_wait(barrier, 2 * tp - 1)
 
-    half = dim // 2
-    width = half // PIECES
+    width = depth // 2
 
     def columns(c, k):
-        return pl.ds(pl.multiple_of(c * half + k * width, LANES), width)
+        return pl.ds(pl.multiple_of(k * depth + c * width, LANES), width)
 
     def across(k):
         return pltpu.make_async_remote_copy(
@@ -97,18 +117,18 @@
     ids_copy = pltpu.make_async_remote_copy(src_ref=ids, dst_ref=far_ids, send_sem=i_send, recv_sem=i_recv,
                                             device_id={'dp': mate, 'tp': me}, device_id_type=MESH)
     ids_copy.start()
-    for k in range(PIECES):
-        across(k).start()
-
-    nb[...] = jnp.zeros_like(nb)
+    across(0).start()
+
     whole = rows // 16 * 16
 
-    def pack(base, src):
-        nb[pl.ds(base, whole), :] = src[0:whole, :].astype(jnp.bfloat16)
-        rest = src[whole:rows, :]
-        nb[pl.ds(base + whole, 16), :] = jnp.concatenate([rest, jnp.zeros_like(rest)], axis=0).astype(jnp.bfloat16)
-
-    pack(0, near_f32)
+    def pack(base, src, start, width):
+        span = pl.ds(start, width)
+        nb[pl.ds(base, whole), span] = src[0:whole, span].astype(jnp.bfloat16)
+        rest = src[whole:rows, span]
+        nb[pl.ds(base + whole, 16), span] = jnp.concatenate([rest, jnp.zeros_like(rest)], axis=0).astype(jnp.bfloat16)
+        nb[pl.ds(base + whole + 16, LANES - whole - 16), span] = jnp.zeros((LANES - whole - 16, width), jnp.bfloat16)
+
+    pack(0, near_f32, 0, dim)
 
     lane = lax.broadcasted_iota(jnp.int32, (seqs, LANES), 1)
     sub = lax.broadcasted_iota(jnp.int32, (seqs, LANES), 0)
@@ -120,9 +140,9 @@
         row = jnp.sum(jnp.where(lane % seqs == sub, spread, 0), axis=0, keepdims=True)
         return jnp.broadcast_to(jnp.where(lane[:1] < drafts * seqs, row, -1), (seqs, LANES)) - sub
 
-    def stats(carry, id_rel, buf, base, first, count):
+    def stats(carry, id_rel, buf, row, base, first, count):
         m, s, w, p = carry
-        z = [logits[buf, pl.ds(8 * j, 8), base:base + LANES] for j in range(count // 8)]
+        z = [buf[row + 8 * j:row + 8 * j + 8, base:base + LANES] for j in range(count // 8)]
         tree = list(z)
         while len(tree) > 1:
             tree = [jnp.maximum(tree[i], tree[i + 1]) if i + 1 < len(tree) else tree[i] for i in range(0, len(tree), 2)]
@@ -145,48 +165,85 @@
     fresh = (low, zero, zero, zero)
     near_id = id_grid(ids)
 
-    def refill(block, slot):
-        @pl.when(block < blocks)
-        def _():
-            load(block, slot).start()
-
-        @pl.when(block == blocks)
-        def _():
-            load_tail(slot).start()
-
-    def pair(block, near, far=None, second=BLOCK):
-        wide = LANES if far is None else 2 * LANES
-        counts = (BLOCK, second)
-        slots = [lax.rem(block + u, SLOTS) for u in range(2)]
-        load(block, slots[0]).wait()
-        if second == BLOCK:
-            load(block + 1, slots[1]).wait()
-        else:
-            load_tail(slots[1]).wait()
-        for u in range(2):
-            logits[u, 0:counts[u], 0:wide] = lax.dot_general(ring[slots[u], 0:counts[u]], nb[0:wide], NT, preferred_element_type=F32)
-        for u in range(2):
-            refill(block + u + SLOTS, slots[u])
-        for u in range(2):
-            first = first_col(block + u)
-            near = stats(near, near_id, u, 0, first, counts[u])
-            if far is not None:
-                far = stats(far, far_id, u, LANES, first, counts[u])
-        return near, far
-
-    near = lax.fori_loop(0, ALONE // 2, lambda i, c: pair(2 * i, c)[0], fresh)
-    for k in range(PIECES):
-        across(k).wait_recv()
-        onward(k).start()
+    def product(slot, count, lanes, half):
+        return lax.dot_general(ring[slot, 0:count], nb[0:lanes, half * depth:(half + 1) * depth], NT, preferred_element_type=F32)
+
+    def arrive(unit, counts):
+        slots = [lax.rem(unit + u, SLOTS) for u in range(len(counts))]
+        for u, count in enumerate(counts):
+            load(unit + u, slots[u], count).wait()
+        for u in range(len(counts)):
+            ahead = unit + u + SLOTS - TRIP
+            begin(ahead, lax.rem(ahead, SLOTS))
+        return slots
+
+    def alone_trip(i, carry):
+        unit = i * TRIP
+        slots = arrive(unit, [BLOCK] * TRIP)
+        for b in range(TRIP // HALVES):
+            logits[b * BLOCK:(b + 1) * BLOCK, 0:LANES] = sum(product(slots[b * HALVES + h], BLOCK, LANES, h) for h in range(HALVES))
+        for b in range(TRIP // HALVES):
+            block = i * (TRIP // HALVES) + b
+            carry = stats(carry, near_id, logits, b * BLOCK, 0, block * BLOCK, BLOCK)
+
+        @pl.when(i == 1)
+        def _():
+            across(0).wait_send()
+            across(1).start()
+
+        @pl.when(i == 2)
+        def _():
+            across(0).wait_recv()
+            onward(0).start()
+
+        return carry
+
+    near = lax.fori_loop(0, lone // TRIP, alone_trip, fresh)
     ids_copy.wait_recv()
     far_id = id_grid(far_ids)
-    for k in range(PIECES):
-        landing(k).wait_recv()
-    pack(LANES, far_f32)
-
-    together = blocks - ALONE
-    near, far = lax.fori_loop(0, together // 2, lambda i, c: pair(ALONE + 2 * i, *c), (near, fresh))
-    near, far = pair(jnp.int32(blocks - 1), near, far, tail)
+    landing(0).wait_recv()
+    pack(LANES, far_f32, 0, depth)
+
+    def first_half(j, counts):
+        unit = lone + j
+        slots = arrive(unit, counts)
+        for u, count in enumerate(counts):
+            part[pl.ds(pl.multiple_of((j + u) * BLOCK, BLOCK), count)] = product(slots[u], count, 2 * LANES, 0)
+
+    def second_half(j, counts, near, far):
+        unit = lone + sharing + j
+        slots = arrive(unit, counts)
+        def settle(u, near, far):
+            first = alone + side * share + (j + u) * BLOCK
+            near = stats(near, near_id, logits, u * BLOCK, 0, first, counts[u])
+            return near, stats(far, far_id, logits, u * BLOCK, LANES, first, counts[u])
+
+        for u, count in enumerate(counts):
+            span = pl.ds(pl.multiple_of((j + u) * BLOCK, BLOCK), count)
+            logits[u * BLOCK:u * BLOCK + count] = part[span] + product(slots[u], count, 2 * LANES, 1)
+            if u:
+                near, far = settle(u - 1, near, far)
+        return settle(len(counts) - 1, near, far)
+
+    trips = (sharing - 1) // TRIP
+    rest = [BLOCK] * (sharing - 1 - trips * TRIP) + [last]
+
+    def first_trip(i, carry):
+        first_half(i * TRIP, [BLOCK] * TRIP)
+
+        @pl.when(i == 1)
+        def _():
+            across(1).wait_recv()
+            onward(1).start()
+
+        return carry
+
+    lax.fori_loop(0, trips, first_trip, 0)
+    first_half(jnp.int32(trips * TRIP), rest)
+    landing(1).wait_recv()
+    pack(LANES, far_f32, depth, depth)
+    near, far = lax.fori_loop(0, trips, lambda i, c: second_half(i * TRIP, [BLOCK] * TRIP, *c), (near, fresh))
+    near, far = second_half(jnp.int32(trips * TRIP), rest, near, far)
 
     def fold(carry):
         m, s, w, p = carry
@@ -196,7 +253,7 @@
         w = jnp.sum(keep * (w + s * drop), axis=0, keepdims=True)
         s = jnp.sum(keep * s, axis=0, keepdims=True)
         p = jnp.sum(p, axis=0, keepdims=True)
-        return jnp.where(sub == 0, top, jnp.where(sub == 1, s, jnp.where(sub == 2, w, jnp.where(sub == 3, p, 0.0))))
+        return jnp.where(sub == 0, top, jnp.where(sub == 1, s, jnp.where(sub == 2, w, p)))[0:4]
 
     own = side * tp + me
     msgs[2 * tp] = fold(far)
@@ -227,8 +284,8 @@
     out_ref[...] = msgs[0:2 * tp]
     for copy in sends:
         copy.wait_send()
-    for k in range(PIECES):
-        across(k).wait_send()
+    across(1).wait_send()
+    for k in range(HALVES):
         onward(k).wait_send()
     ids_copy.wait_send()
 
@@ -276,6 +333,7 @@
         seqs, steps, dim = hidden.shape
         rows = steps * seqs
         drafts = draft_ids.shape[1]
+        cols = head_w.shape[1]
         anywhere = pl.BlockSpec(memory_space=pl.ANY)
         vmem = pl.BlockSpec(memory_space=pltpu.VMEM)
         dma = pltpu.SemaphoreType.DMA
@@ -283,7 +341,7 @@
             functools.partial(kernel, tp),
             in_specs=[anywhere] * 4,
             out_specs=vmem,
-            out_shape=jax.ShapeDtypeStruct((2 * tp, 8, LANES), F32),
+            out_shape=jax.ShapeDtypeStruct((2 * tp, 4, LANES), F32),
             scratch_shapes=[
                 pltpu.VMEM((steps, seqs, dim), jnp.bfloat16),
                 pltpu.VMEM((seqs, drafts), jnp.int32),
@@ -292,12 +350,13 @@
                 pltpu.VMEM((rows, dim), F32),
                 pltpu.VMEM((rows, dim), F32),
                 pltpu.VMEM((2 * LANES, dim), jnp.bfloat16),
-                pltpu.VMEM((SLOTS, BLOCK, dim), jnp.bfloat16),
-                pltpu.VMEM((2, BLOCK, 2 * LANES), F32),
-                pltpu.VMEM((2 * tp + 1, 8, LANES), F32),
+                pltpu.VMEM((SLOTS, BLOCK, dim // HALVES), jnp.bfloat16),
+                pltpu.VMEM((TRIP * BLOCK, 2 * LANES), F32),
+                pltpu.VMEM((pl.cdiv((cols - ALONE * BLOCK) // 2, BLOCK) * BLOCK, 2 * LANES), F32),
+                pltpu.VMEM((2 * tp + 1, 4, LANES), F32),
                 dma, dma, dma,
                 dma((SLOTS,)),
-                dma((PIECES,)), dma((PIECES,)), dma((PIECES,)), dma((PIECES,)),
+                dma((HALVES,)), dma((HALVES,)), dma((HALVES,)), dma((HALVES,)),
                 dma, dma,
                 dma((2 * tp,)), dma((2 * tp,)),
             ],

time: 48.9 us -> 42 us (0.86)
  Pallas kernels: 48.1 us -> 41.3 us
    pallas_call x1, Pallas kernels: 46.5 us -> 39.8 us  [per_device(): pl.pallas_call(functools.partial(kernel, tp), in_specs=[anywhere] * 4, ou...]
where the time goes in v3:
time: 42 us; the launch traced here: 41.9 us
  Pallas kernels  41.3 us (98%)
  between operations  0.64 us (2%)
    pallas_call x1, Pallas kernels, per_device(): pl.pallas_call(functools.partial(kernel, tp), in_specs=[anywhere] * 4, ou...  39.8 us
    pallas_call x1, Pallas kernels, per_device(): pl.pallas_call(finish, in_specs=[vmem], out_specs=[vmem] * 3, out_shape=[...  1.51 us

profile of v3, /device:TPU:81, one launch (start us, length us, event | category | flops | bytes accessed | tf_op | source)
XLA Modules:
  0.0 41.9 jit_solution(15462230104638367586)
XLA Ops:
  0.6 39.8 %shard_map.67.parts_ref = f32[16,4,128]{2,1,0:T(4,128)} custom-call(bf16[9,8,4096]{2,1,0:T(8,128)(2,1)} %bitcast.3, s32[8,8]{1,0:T(8,128)} %ids_hbm.1, bf16[32,128]{1,0:T(8,128)(2,1)} %bitcast.4, bf16[16032,4096]{1,0:T(8,128)(2,1)} %bitcast.2.wt_hbm), custom_call_target="tpu_custom_call" | custom-call | tf_op jit(solution)/shard_map/pallas_call | solution.py:340
  40.4 1.5 %shard_map.68 = (f32[8,8]{1,0:T(8,128)}, f32[8,9]{1,0:T(8,128)}, f32[8,9]{1,0:T(8,128)}) custom-call(f32[16,4,128]{2,1,0:T(4,128)} %shard_map.67.parts_ref), custom_call_target="tpu_custom_call" | custom-call | tf_op jit(solution)/shard_map/pallas_call | solution.py:365

commit v4 on v3

--- a/solution.py
+++ b/solution.py
@@ -9,10 +9,10 @@
 
 NORM_EPS = 1e-5
 BLOCK = 512
-SLOTS = 12
-ALONE = 8
-HALVES = 2
-TRIP = 4
+SLOTS = 24
+ALONE = 4
+PARTS = 4
+TRIP = 8
 LANES = 128
 NT = (((1,), (1,)), ((), ()))
 F32 = jnp.float32
@@ -31,9 +31,9 @@
     tail = share % BLOCK
     sharing = share // BLOCK + (tail > 0)
     last = tail or BLOCK
-    depth = dim // HALVES
-    lone = ALONE * HALVES
-    units = lone + sharing * HALVES
+    depth = dim // PARTS
+    lone = ALONE * PARTS
+    units = lone + sharing * PARTS
     group, me = lax.axis_index('dp'), lax.axis_index('tp')
     side = lax.rem(group, 2)
     mate = group + 1 - 2 * side
@@ -47,10 +47,10 @@
 
     def place(unit):
         own, far = unit < lone, unit - lone
-        half = jnp.where(own, lax.rem(unit, HALVES), far // sharing)
-        block = jnp.where(own, unit // HALVES, lax.rem(far, sharing))
+        piece = jnp.where(own, lax.rem(unit, PARTS), far // sharing)
+        block = jnp.where(own, unit // PARTS, lax.rem(far, sharing))
         col = block * BLOCK + jnp.where(own, 0, alone + side * share)
-        return pl.multiple_of(col, 16), pl.multiple_of(half * depth, LANES)
+        return pl.multiple_of(col, 16), pl.multiple_of(piece * depth, LANES)
 
     def load(unit, slot, count=BLOCK):
         col, start = place(unit)
@@ -118,7 +118,6 @@
                                             device_id={'dp': mate, 'tp': me}, device_id_type=MESH)
     ids_copy.start()
     across(0).start()
-
     whole = rows // 16 * 16
 
     def pack(base, src, start, width):
@@ -165,8 +164,9 @@
     fresh = (low, zero, zero, zero)
     near_id = id_grid(ids)
 
-    def product(slot, count, lanes, half):
-        return lax.dot_general(ring[slot, 0:count], nb[0:lanes, half * depth:(half + 1) * depth], NT, preferred_element_type=F32)
+    def product(slot, count, lanes, piece):
+        span = pl.ds(piece * depth if isinstance(piece, int) else pl.multiple_of(piece * depth, LANES), depth)
+        return lax.dot_general(ring[slot, 0:count], nb[0:lanes, span], NT, preferred_element_type=F32)
 
     def arrive(unit, counts):
         slots = [lax.rem(unit + u, SLOTS) for u in range(len(counts))]
@@ -180,70 +180,70 @@
     def alone_trip(i, carry):
         unit = i * TRIP
         slots = arrive(unit, [BLOCK] * TRIP)
-        for b in range(TRIP // HALVES):
-            logits[b * BLOCK:(b + 1) * BLOCK, 0:LANES] = sum(product(slots[b * HALVES + h], BLOCK, LANES, h) for h in range(HALVES))
-        for b in range(TRIP // HALVES):
-            block = i * (TRIP // HALVES) + b
+        for b in range(TRIP // PARTS):
+            logits[b * BLOCK:(b + 1) * BLOCK, 0:LANES] = sum(product(slots[b * PARTS + h], BLOCK, LANES, h) for h in range(PARTS))
+        for b in range(TRIP // PARTS):
+            block = i * (TRIP // PARTS) + b
             carry = stats(carry, near_id, logits, b * BLOCK, 0, block * BLOCK, BLOCK)
 
-        @pl.when(i == 1)
-        def _():
-            across(0).wait_send()
-            across(1).start()
-
-        @pl.when(i == 2)
-        def _():
-            across(0).wait_recv()
-            onward(0).start()
-
+        across(i + 1).start()
         return carry
 
     near = lax.fori_loop(0, lone // TRIP, alone_trip, fresh)
+    across(0).wait_recv()
+    onward(0).start()
+    part[...] = jnp.zeros_like(part)
     ids_copy.wait_recv()
     far_id = id_grid(far_ids)
     landing(0).wait_recv()
     pack(LANES, far_f32, 0, depth)
 
-    def first_half(j, counts):
-        unit = lone + j
-        slots = arrive(unit, counts)
+    sizes = [BLOCK] * (sharing - 1) + [last]
+    middle = (sharing + 1) // 2
+    runs = ((0, sizes[:middle]), (middle, sizes[middle:]))
+
+    def gather(p, run):
+        j, counts = run
+        slots = arrive(lone + p * sharing + j, counts)
         for u, count in enumerate(counts):
-            part[pl.ds(pl.multiple_of((j + u) * BLOCK, BLOCK), count)] = product(slots[u], count, 2 * LANES, 0)
-
-    def second_half(j, counts, near, far):
-        unit = lone + sharing + j
-        slots = arrive(unit, counts)
+            span = pl.ds((j + u) * BLOCK, count)
+            part[span] = part[span] + product(slots[u], count, 2 * LANES, p)
+
+    def phase(p, carry):
+        gather(p, runs[0])
+        across(p + 1).wait_recv()
+        onward(p + 1).start()
+
+        @pl.when(p + ALONE * PARTS // TRIP + 1 < PARTS)
+        def _():
+            across(p + ALONE * PARTS // TRIP + 1).start()
+
+        gather(p, runs[1])
+        landing(p + 1).wait_recv()
+        pack(LANES, far_f32, pl.multiple_of((p + 1) * depth, LANES), depth)
+        return carry
+
+    lax.fori_loop(0, PARTS - 1, phase, 0)
+
+    def conclude(run, near, far):
+        j, counts = run
+        slots = arrive(jnp.int32(lone + (PARTS - 1) * sharing + j), counts)
+
         def settle(u, near, far):
             first = alone + side * share + (j + u) * BLOCK
             near = stats(near, near_id, logits, u * BLOCK, 0, first, counts[u])
             return near, stats(far, far_id, logits, u * BLOCK, LANES, first, counts[u])
 
         for u, count in enumerate(counts):
-            span = pl.ds(pl.multiple_of((j + u) * BLOCK, BLOCK), count)
-            logits[u * BLOCK:u * BLOCK + count] = part[span] + product(slots[u], count, 2 * LANES, 1)
+            span = pl.ds((j + u) * BLOCK, count)
+            logits[u * BLOCK:u * BLOCK + count] = part[span] + product(slots[u], count, 2 * LANES, PARTS - 1)
             if u:
                 near, far = settle(u - 1, near, far)
         return settle(len(counts) - 1, near, far)
 
-    trips = (sharing - 1) // TRIP
-    rest = [BLOCK] * (sharing - 1 - trips * TRIP) + [last]
-
-    def first_trip(i, carry):
-        first_half(i * TRIP, [BLOCK] * TRIP)
-
-        @pl.when(i == 1)
-        def _():
-            across(1).wait_recv()
-            onward(1).start()
-
-        return carry
-
-    lax.fori_loop(0, trips, first_trip, 0)
-    first_half(jnp.int32(trips * TRIP), rest)
-    landing(1).wait_recv()
-    pack(LANES, far_f32, depth, depth)
-    near, far = lax.fori_loop(0, trips, lambda i, c: second_half(i * TRIP, [BLOCK] * TRIP, *c), (near, fresh))
-    near, far = second_half(jnp.int32(trips * TRIP), rest, near, far)
+    near, far = near, fresh
+    for run in runs:
+        near, far = conclude(run, near, far)
 
     def fold(carry):
         m, s, w, p = carry
@@ -284,8 +284,8 @@
     out_ref[...] = msgs[0:2 * tp]
     for copy in sends:
         copy.wait_send()
-    across(1).wait_send()
-    for k in range(HALVES):
+    for k in range(PARTS):
+        across(k).wait_send()
         onward(k).wait_send()
     ids_copy.wait_send()
 
@@ -334,7 +334,7 @@
         rows = steps * seqs
         drafts = draft_ids.shape[1]
         cols = head_w.shape[1]
-        anywhere = pl.BlockSpec(memory_space=pl.ANY)
+        anywhere = pl.BlockSpec(memory_space=pltpu.HBM)
         vmem = pl.BlockSpec(memory_space=pltpu.VMEM)
         dma = pltpu.SemaphoreType.DMA
         parts = pl.pallas_call(
@@ -350,24 +350,26 @@
                 pltpu.VMEM((rows, dim), F32),
                 pltpu.VMEM((rows, dim), F32),
                 pltpu.VMEM((2 * LANES, dim), jnp.bfloat16),
-                pltpu.VMEM((SLOTS, BLOCK, dim // HALVES), jnp.bfloat16),
+                pltpu.VMEM((SLOTS, BLOCK, dim // PARTS), jnp.bfloat16),
                 pltpu.VMEM((TRIP * BLOCK, 2 * LANES), F32),
                 pltpu.VMEM((pl.cdiv((cols - ALONE * BLOCK) // 2, BLOCK) * BLOCK, 2 * LANES), F32),
                 pltpu.VMEM((2 * tp + 1, 4, LANES), F32),
                 dma, dma, dma,
                 dma((SLOTS,)),
-                dma((HALVES,)), dma((HALVES,)), dma((HALVES,)), dma((HALVES,)),
+                dma((PARTS,)), dma((PARTS,)), dma((PARTS,)), dma((PARTS,)),
                 dma, dma,
                 dma((2 * tp,)), dma((2 * tp,)),
             ],
-            compiler_params=pltpu.CompilerParams(collective_id=0, has_side_effects=True, vmem_limit_bytes=60 * 2**20),
-        )(hidden.transpose(1, 0, 2), draft_ids, norm_gain.reshape(dim // LANES, LANES), head_w.T)
+            compiler_params=pltpu.CompilerParams(collective_id=0, has_side_effects=True, vmem_limit_bytes=46 * 2**20),
+        )(*(pltpu.with_memory_space_constraint(x, pltpu.HBM) for x in (
+            hidden.transpose(1, 0, 2), draft_ids, norm_gain.reshape(dim // LANES, LANES), head_w.T)))
         return pl.pallas_call(
             finish,
             in_specs=[vmem],
             out_specs=[vmem] * 3,
             out_shape=[jax.ShapeDtypeStruct((seqs, drafts), F32), jax.ShapeDtypeStruct((seqs, steps), F32),
                        jax.ShapeDtypeStruct((seqs, steps), F32)],
+            compiler_params=pltpu.CompilerParams(vmem_limit_bytes=4 * 2**20),
         )(parts)
 
     specs_in = (P('dp', None, None), P('dp', None), P(None), P(None, 'tp'))

time: 42 us -> 40.6 us (0.967)
  Pallas kernels: 41.3 us -> 39.9 us
    pallas_call x1, Pallas kernels: 1.51 us -> 0.75 us  [per_device(): pl.pallas_call(finish, in_specs=[vmem], out_specs=[vmem] * 3, out_shape=[...]
    pallas_call x1, Pallas kernels: 39.8 us -> 39.1 us  [per_device(): pl.pallas_call(functools.partial(kernel, tp), in_specs=[anywhere] * 4, ou...]
where the time goes in v4:
time: 40.6 us; the launch traced here: 40.5 us
  Pallas kernels  39.9 us (98%)
  between operations  0.64 us (2%)
    pallas_call x1, Pallas kernels, per_device(): pl.pallas_call(functools.partial(kernel, tp), in_specs=[anywhere] * 4, ou...  39.1 us

profile of v4, /device:TPU:81, one launch (start us, length us, event | category | flops | bytes accessed | tf_op | source)
XLA Modules:
  0.0 40.5 jit_solution(12585511393553542378)
XLA Ops:
  0.6 39.1 %shard_map.67.parts_ref = f32[16,4,128]{2,1,0:T(4,128)S(1)} custom-call(bf16[9,8,4096]{2,1,0:T(8,128)(2,1)} %bitcast.3, s32[8,8]{1,0:T(8,128)} %ids_hbm.1, bf16[32,128]{1,0:T(8,128)(2,1)} %bitcast.4, bf16[16032,4096]{1,0:T(8,128)(2,1)} %bitcast.2.wt_hbm), custom_call_target="tpu_custom_call" | custom-call | tf_op jit(solution)/shard_map/pallas_call | solution.py:340
  39.8 0.8 %shard_map.68 = (f32[8,8]{1,0:T(8,128)}, f32[8,9]{1,0:T(8,128)}, f32[8,9]{1,0:T(8,128)}) custom-call(f32[16,4,128]{2,1,0:T(4,128)S(1)} %shard_map.67.parts_ref), custom_call_target="tpu_custom_call" | custom-call | tf_op jit(solution)/shard_map/pallas_call | solution.py:366
